TPU v7x, 32 devices: a whole 2x2x4 slice. The times are simulated.
32 devices in a mesh: dp: 4 (over y, x), tensor: 8 (over z, core).
Axes of the slice: x: 2, y: 2, z: 4, core: 2. Of those that a mesh axis runs over, the one named last changes fastest.
Arguments:
- queries: bfloat16 [1536, 8192], P('dp', 'tensor'), may hold values from -180 to 180
- keys: bfloat16 [1536, 1024], P('dp'), may hold values from -4.5 to 4.5
- values: bfloat16 [1536, 1024], P('dp'), may hold values from -6 to 6
- grad_out: bfloat16 [1536, 8192], P('dp', 'tensor'), may hold values from -3 to 3
- weight: float32 [8192, 8192], P('dp', 'tensor'), as said below
- first_code: bfloat16 [8192, 8192], P('dp', 'tensor'), may hold values from -1 to 1, as said below
- first_rows: float32 [8192], P('dp'), may hold values from 0.2 to 5
- first_cols: float32 [8192], P('tensor'), may hold values from 0.2 to 5
- second_code: bfloat16 [8192, 8192], P('dp', 'tensor'), may hold values from 0 to 1, as said below
- second_rows: float32 [8192], P('dp'), may hold values from 0.5 to 20
- second_cols: float32 [8192], P('tensor'), may hold values from 0.5 to 20
Outputs:
- grad_queries: bfloat16 [1536, 8192], P('dp', 'tensor')
- new_weight: float32 [8192, 8192], P('dp', 'tensor')
- next_first_code: bfloat16 [8192, 8192], P('dp', 'tensor')
- next_first_rows: float32 [8192], P('dp')
- next_first_cols: float32 [8192], P('tensor')
- next_second_code: bfloat16 [8192, 8192], P('dp', 'tensor')
- next_second_rows: float32 [8192], P('dp')
- next_second_cols: float32 [8192], P('tensor')
Inputs may be any that keep to these rules, and one draw needn't show every extreme that they name: `weight`: rows 8192 onward are zero. `first_code`: rows 8192 onward are zero. `second_code`: rows 8192 onward are zero; all other entries are 0.05 or more.
All inputs are finite; a program needn't handle non-finite values.
Results may differ from a plain program's by a relative error of at most 0.023.
Values may be sent and summed in bfloat16 or wider, within the bound.
A program may use at most 128 MiB of HBM per device.

v0:
```python
import jax
import jax.numpy as jnp
from jax import lax
from jax.sharding import PartitionSpec as P

H = 64
KVH = 8
HD = 128
beta_first = 0.9
beta_second = 0.95
learning = 0.01
decay_rate = 0.1
adam_eps = 1e-08
code_eps = 1e-06
correct_first = 1.0 - 0.9**10
correct_second = 1.0 - 0.95**10


def attend(queries, key_sel, value_sel, heads_dev):
    length = queries.shape[0]
    query_heads = queries.reshape(length, heads_dev, HD)
    scores = jnp.einsum(
        "qhd,kd->hqk", query_heads, key_sel, preferred_element_type=jnp.float32
    ) * HD ** (-0.5)
    future = lax.broadcasted_iota(jnp.int32, (length, length), 1) > lax.broadcasted_iota(
        jnp.int32, (length, length), 0
    )
    scores = jnp.where(future[None], -1e30, scores)
    highest = jnp.max(scores, axis=-1, keepdims=True)
    exponent = jnp.exp(scores - highest)
    probabilities = exponent / jnp.sum(exponent, axis=-1, keepdims=True)
    weights_half = probabilities.astype(jnp.bfloat16)
    attended = jnp.einsum(
        "hqk,kd->qhd", weights_half, value_sel, preferred_element_type=jnp.float32
    )
    return (probabilities, attended.astype(jnp.bfloat16).reshape(length, heads_dev * HD))


def attend_back(probabilities, attended, grad_half, key_sel, value_sel, heads_dev):
    length = grad_half.shape[0]
    grad_heads = grad_half.reshape(length, heads_dev, HD)
    grad_probs = jnp.einsum(
        "qhd,kd->hqk", grad_heads, value_sel, preferred_element_type=jnp.float32
    )
    row_dot = jnp.sum(
        grad_heads.astype(jnp.float32)
        * attended.reshape(length, heads_dev, HD).astype(jnp.float32),
        axis=-1,
    )
    grad_scores = (probabilities * (grad_probs - row_dot.T[:, :, None])).astype(jnp.bfloat16)
    grad_query = jnp.einsum(
        "hqk,kd->qhd", grad_scores, key_sel, preferred_element_type=jnp.float32
    ) * HD ** (-0.5)
    return grad_query.astype(jnp.bfloat16).reshape(length, heads_dev * HD)


def per_device(
    queries,
    keys,
    values,
    grad_out,
    weight,
    first_code,
    first_rows,
    first_cols,
    second_code,
    second_rows,
    second_cols,
):
    dp_count = lax.axis_size("dp")
    cols_dev = queries.shape[1]
    heads_dev = cols_dev // HD
    rows_dev = weight.shape[0]
    width_pad = dp_count * rows_dev
    tensor_index = lax.axis_index("tensor")
    kv_start = tensor_index * heads_dev // (H // KVH) * HD
    weight_half = weight.astype(jnp.bfloat16)
    full_grad = lax.all_gather(grad_out, "tensor", axis=1, tiled=True)
    padded = jnp.pad(full_grad, ((0, 0), (0, width_pad - full_grad.shape[1])))
    key_sel = lax.dynamic_slice_in_dim(keys, kv_start, HD, 1)
    value_sel = lax.dynamic_slice_in_dim(values, kv_start, HD, 1)
    probabilities, attended = attend(queries, key_sel, value_sel, heads_dev)
    block = padded
    grad_att = jnp.dot(
        block,
        lax.all_gather(weight_half, "dp", axis=0, tiled=True),
        preferred_element_type=jnp.float32,
    )
    block = padded
    weight_grad = lax.psum_scatter(
        jnp.einsum("sc,sh->ch", block, attended, preferred_element_type=jnp.float32).astype(
            jnp.bfloat16
        ),
        "dp",
        scatter_dimension=0,
        tiled=True,
    ).astype(jnp.float32)
    grad_half = grad_att.astype(jnp.bfloat16)
    grad_queries = attend_back(probabilities, attended, grad_half, key_sel, value_sel, heads_dev)
    first = first_code.astype(jnp.float32) * jnp.minimum(first_rows[:, None], first_cols[None, :])
    second = second_code.astype(jnp.float32) * jnp.minimum(
        second_rows[:, None], second_cols[None, :]
    )
    first_new = beta_first * first + (1.0 - beta_first) * weight_grad
    second_new = beta_second * second + (1.0 - beta_second) * weight_grad * weight_grad
    step_size = first_new / correct_first / (jnp.sqrt(second_new / correct_second) + adam_eps)
    new_weight = weight - learning * (step_size + decay_rate * weight)
    first_abs = jnp.abs(first_new)
    second_abs = jnp.abs(second_new)
    local_rows_max = jnp.stack([jnp.max(first_abs, axis=1), jnp.max(second_abs, axis=1)])
    local_cols_max = jnp.stack([jnp.max(first_abs, axis=0), jnp.max(second_abs, axis=0)])
    rows_mine = lax.pmax(local_rows_max, "tensor")
    cols_mine = lax.pmax(local_cols_max, "dp")
    next_first_code = (
        first_new / (jnp.minimum(rows_mine[0][:, None], cols_mine[0][None, :]) + code_eps)
    ).astype(jnp.bfloat16)
    next_second_code = (
        second_new / (jnp.minimum(rows_mine[1][:, None], cols_mine[1][None, :]) + code_eps)
    ).astype(jnp.bfloat16)
    return (
        grad_queries,
        new_weight,
        next_first_code,
        rows_mine[0],
        cols_mine[0],
        next_second_code,
        rows_mine[1],
        cols_mine[1],
    )


def solution(mesh):
    return jax.shard_map(
        per_device,
        mesh=mesh,
        in_specs=(
            P("dp", "tensor"),
            P("dp", None),
            P("dp", None),
            P("dp", "tensor"),
            P("dp", "tensor"),
            P("dp", "tensor"),
            P("dp"),
            P("tensor"),
            P("dp", "tensor"),
            P("dp"),
            P("tensor"),
        ),
        out_specs=(
            P("dp", "tensor"),
            P("dp", "tensor"),
            P("dp", "tensor"),
            P("dp"),
            P("tensor"),
            P("dp", "tensor"),
            P("dp"),
            P("tensor"),
        ),
        check_vma=False,
    )
```

profile of v0, /device:TPU:0, one launch (start us, length us, event | category | flops | bytes accessed | tf_op | source)
XLA Modules:
  0.0 510.6 jit_solution(8589471572485193456)
XLA Ops:
  7.2 0.0 copy-start
  7.2 0.0 all-gather.3.cloned.1.call-start
  7.2 0.7 all-gather.3.cloned.1.call-update
  7.9 0.0 copy-start.1
  7.9 0.0 all-gather.5.cloned.1.call-start
  8.0 6.1 %convert_element_type.51 = bf16[2048,1024]{1,0:T(8,128)(2,1)} convert(f32[2048,1024]{1,0:T(8,128)} %param.15) | non-fusion elementwise | flops 2097152 | bytes 12582912 | tf_op jit(solution)/shard_map/convert_element_type | solution.py:77
  14.1 0.0 all-gather.5.cloned.1.call-update
  14.1 0.0 reduce-scatter.2.cloned.1.call-start
  14.2 0.0 copy-done
  14.3 0.0 copy-done.1
  14.3 0.8 fusion.21
  15.1 3.7 fusion.42
  18.7 58.3 %all-gather.3.cloned.1.call-done = bf16[384,8192]{1,0:T(8,128)(2,1)} async-done(((bf16[384,1024]{1,0:T(8,128)(2,1)}), bf16[384,8192]{1,0:T(8,128)(2,1)}) %all-gather.3.cloned.1.call-update) | async-done | bytes 6291472 | tf_op jit(solution)/shard_map/all_gather | solution.py:78
  77.0 158.4 %all-gather.5.cloned.1.call-done = bf16[8192,1024]{1,0:T(8,128)(2,1)} async-done(((bf16[2048,1024]{1,0:T(8,128)(2,1)}), bf16[8192,1024]{1,0:T(8,128)(2,1)}) %all-gather.5.cloned.1.call-update) | async-done | bytes 16777232 | tf_op jit(solution)/shard_map/all_gather | solution.py:86
  235.4 12.1 %convolution_convert_fusion = bf16[384,1024]{1,0:T(8,128)(2,1)S(1)} fusion(bf16[384,8192]{1,0:T(8,128)(2,1)} %all-gather.3.cloned.1.call-done, bf16[8192,1024]{1,0:T(8,128)(2,1)} %all-gather.5.cloned.1.call-done), kind=kOutput, calls=%fused_computation.30 | convolution fusion | flops 6442844160 | bytes 23855104 | tf_op jit(solution)/shard_map/dot_general | solution.py:84
  247.5 0.4 copy.37
  247.9 3.0 multiply_reduce_fusion
  250.9 14.5 %convert_bitcast_fusion = bf16[8192,1024]{0,1:T(8,128)(2,1)} fusion(bf16[384,1024]{0,1:T(8,128)(2,1)S(1)} %bitcast.82, bf16[384,8192]{1,0:T(8,128)(2,1)} %all-gather.3.cloned.1.call-done), kind=kOutput, calls=%fused_computation.1 | convolution fusion | flops 6450839552 | bytes 23855104 | tf_op jit(solution)/shard_map/sc,sh->ch/dot_general | solution.py:91
  265.4 0.0 reduce-scatter.2.cloned.1.call-update
  265.4 9.4 %copy.28 = f32[2048,1024]{0,1:T(8,128)} copy(f32[2048,1024]{1,0:T(8,128)} %param.15) | data formatting | bytes 16777216 | tf_op args[4]
  274.8 6.4 %copy.25 = bf16[2048,1024]{0,1:T(8,128)(2,1)} copy(bf16[2048,1024]{1,0:T(8,128)(2,1)} %param.16) | data formatting | bytes 8388608 | tf_op args[5]
  281.2 6.5 %copy.26 = bf16[2048,1024]{0,1:T(8,128)(2,1)} copy(bf16[2048,1024]{1,0:T(8,128)(2,1)} %param.19) | data formatting | bytes 8388608 | tf_op args[8]
  287.7 0.0 copy-start.4
  287.7 0.0 copy-start.5
  287.7 0.0 copy-start.8
  287.7 0.0 copy-start.9
  287.7 3.7 multiply_convert_fusion
  291.5 1.2 copy.29
  292.6 126.6 %reduce-scatter.2.cloned.1.call-done = bf16[2048,1024]{0,1:T(8,128)(2,1)} async-done(((bf16[8192,1024]{0,1:T(8,128)(2,1)}), bf16[2048,1024]{0,1:T(8,128)(2,1)}) %reduce-scatter.2.cloned.1.call-update) | async-done | bytes 4194320 | tf_op jit(solution)/shard_map/reduce_scatter | solution.py:90
  419.3 0.0 copy-done.4
  419.3 0.0 copy-done.5
  419.3 0.0 copy-done.8
  419.3 0.0 copy-done.9
  419.3 15.6 %abs_reduce_fusion.3 = (f32[2048]{0:T(1024)S(1)}, f32[1024]{0:T(1024)S(1)}, f32[1024]{0:T(1024)S(1)}, f32[2048]{0:T(1024)S(1)}, f32[2048,1024]{0,1:T(8,128)}) fusion(bf16[2048,1024]{0,1:T(8,128)(2,1)} %reduce-scatter.2.cloned.1.call-done, f32[1024]{0:T(1024)S(1)} %copy-done.8, f32[2048]{0:T(1024)S(1)} %copy-done.4, bf16[2048,1024]{0,1:T(8,128)(2,1)} %copy.25, ...), kind=kLoop, calls=%fused_computation.12 | loop fusion | flops 58714112 | bytes 29409280 | tf_op jit(solution)/shard_map/reduce_max | solution.py:110
  434.9 9.2 %copy.30 = f32[2048,1024]{1,0:T(8,128)} copy(f32[2048,1024]{0,1:T(8,128)} %get-tuple-element.22) | data formatting | bytes 16777216
  444.2 9.1 %pmax.15 = f32[2,1024]{1,0:T(2,128)S(1)} all-reduce(f32[2,1024]{1,0:T(2,128)S(1)} %pad_maximum_fusion.1), channel_id=1, replica_groups=mesh['dp'=4,'tensor'=8] {'dp'}, use_global_device_ids=true, to_apply=%region_9.10 | all-reduce | flops 2048 | bytes 16384 | tf_op jit(solution)/shard_map/pmax | solution.py:113
  453.3 0.0 copy-start.6
  453.3 0.0 copy-start.7
  453.4 26.4 %pmax.14 = f32[2,2048]{1,0:T(2,128)S(1)} all-reduce(f32[2,2048]{1,0:T(2,128)S(1)} %pad_maximum_fusion), channel_id=1, replica_groups=mesh['dp'=4,'tensor'=8] {'tensor'}, use_global_device_ids=true, to_apply=%region_6.7 | all-reduce | flops 4096 | bytes 32768 | tf_op jit(solution)/shard_map/pmax | solution.py:112
  479.7 0.0 copy-start.2
  479.7 0.0 copy-start.3
  479.7 11.5 %divide_convert_fusion = (bf16[2048,1024]{0,1:T(8,128)(2,1)}, bf16[2048,1024]{0,1:T(8,128)(2,1)}) fusion(f32[1024]{0:T(1024)S(1)} %bitcast.76, f32[2048]{0:T(1024)S(1)} %bitcast.70, bf16[2048,1024]{0,1:T(8,128)(2,1)} %reduce-scatter.2.cloned.1.call-done, f32[1024]{0:T(1024)S(1)} %copy-done.9, f32[2048]{0:T(1024)S(1)} %copy-done.5, ...), kind=kLoop, calls=%fused_computation.6 | loop fusion | flops 46137344 | bytes 21020672 | tf_op jit(solution)/shard_map/convert_element_type | solution.py:119
  491.3 0.0 copy-done.6
  491.3 0.0 copy-done.7
  491.3 0.0 copy-done.2
  491.3 0.0 copy-done.3
  491.3 6.4 %copy.31 = bf16[2048,1024]{1,0:T(8,128)(2,1)} copy(bf16[2048,1024]{0,1:T(8,128)(2,1)} %get-tuple-element.24) | data formatting | bytes 8388608
  497.7 6.4 %copy.32 = bf16[2048,1024]{1,0:T(8,128)(2,1)} copy(bf16[2048,1024]{0,1:T(8,128)(2,1)} %get-tuple-element.23) | data formatting | bytes 8388608
  (5 shorter events, 0.1 us)
Async XLA Ops:
  7.2 7.1 %copy-start = (bf16[384,1024]{1,0:T(8,128)(2,1)S(1)}, bf16[384,1024]{1,0:T(8,128)(2,1)}, u32[]{:S(2)}) copy-start(bf16[384,1024]{1,0:T(8,128)(2,1)} %param.12) | copy-start | bytes 2359300
  7.2 69.9 %all-gather.3.cloned.1.call-start = ((), (), s32[]{:S(2)}) async-start(), calls=%async_computation.1 | async-start | bytes 7077888 | tf_op jit(solution)/shard_map/all_gather | solution.py:78
  7.9 6.3 %copy-start.1 = (bf16[384,1024]{1,0:T(8,128)(2,1)S(1)}, bf16[384,1024]{1,0:T(8,128)(2,1)}, u32[]{:S(2)}) copy-start(bf16[384,1024]{1,0:T(8,128)(2,1)} %param.11) | copy-start | bytes 2359300
  7.9 227.5 %all-gather.5.cloned.1.call-start = ((), (), s32[]{:S(2)}) async-start(), calls=%async_computation.2 | async-start | bytes 20971520 | tf_op jit(solution)/shard_map/all_gather | solution.py:86
  14.1 405.2 %reduce-scatter.2.cloned.1.call-start = ((), (), s32[]{:S(2)}) async-start(), calls=%async_computation.3 | async-start | bytes 20971520 | tf_op jit(solution)/shard_map/reduce_scatter | solution.py:90
  287.7 131.6 %copy-start.4 = (f32[2048]{0:T(1024)S(1)}, f32[2048]{0:T(1024)}, u32[]{:S(2)}) copy-start(f32[2048]{0:T(1024)} %param.17) | copy-start | bytes 24580
  287.7 131.6 %copy-start.5 = (f32[2048]{0:T(1024)S(1)}, f32[2048]{0:T(1024)}, u32[]{:S(2)}) copy-start(f32[2048]{0:T(1024)} %param.20) | copy-start | bytes 24580
  287.7 131.6 %copy-start.8 = (f32[1024]{0:T(1024)S(1)}, f32[1024]{0:T(1024)}, u32[]{:S(2)}) copy-start(f32[1024]{0:T(1024)} %param.18) | copy-start | bytes 12292
  287.7 131.6 %copy-start.9 = (f32[1024]{0:T(1024)S(1)}, f32[1024]{0:T(1024)}, u32[]{:S(2)}) copy-start(f32[1024]{0:T(1024)} %param.21) | copy-start | bytes 12292
  453.3 38.0 %copy-start.6 = (f32[1,1024]{1,0:T(1,128)}, f32[1,1024]{1,0:T(1,128)S(1)}, u32[]{:S(2)}) copy-start(f32[1,1024]{1,0:T(1,128)S(1)} %get-tuple-element.27) | copy-start | bytes 12292
  453.3 37.9 %copy-start.7 = (f32[1,1024]{1,0:T(1,128)}, f32[1,1024]{1,0:T(1,128)S(1)}, u32[]{:S(2)}) copy-start(f32[1,1024]{1,0:T(1,128)S(1)} %get-tuple-element.28) | copy-start | bytes 12292
  479.7 11.5 %copy-start.2 = (f32[1,2048]{1,0:T(1,128)}, f32[1,2048]{1,0:T(1,128)S(1)}, u32[]{:S(2)}) copy-start(f32[1,2048]{1,0:T(1,128)S(1)} %get-tuple-element.25) | copy-start | bytes 24580
  479.7 11.5 %copy-start.3 = (f32[1,2048]{1,0:T(1,128)}, f32[1,2048]{1,0:T(1,128)S(1)}, u32[]{:S(2)}) copy-start(f32[1,2048]{1,0:T(1,128)S(1)} %get-tuple-element.26) | copy-start | bytes 24580
Sparse Core Ops, SparseCore 0:
  9.6 67.4 all-gather.2
  79.5 155.9 all-gather.4
  265.5 153.7 reduce-scatter.1
where the time goes:
time: 512 us; the launch traced here: 511 us
  waiting for transfers between devices  344 us (67%)
  local copies, waits for them, and re-layouts  46 us (9%)
  other arithmetic  37 us (7%)
  blocking collectives  35.4 us (7%)
  matrix products  34.1 us (7%)
  between operations  13.9 us (3%)
    all_gather x1, waiting for transfers between devices, per_device(): lax.all_gather(weight_half, 'dp', axis=0, tiled=True)  158 us
    reduce_scatter x1, waiting for transfers between devices, per_device(): lax.psum_scatter(jnp.einsum('sc,sh->ch', block, attended, preferred_eleme...  127 us
    all_gather x1, waiting for transfers between devices, per_device(): full_grad = lax.all_gather(grad_out, 'tensor', axis=1, tiled=True)  58.3 us
    unnamed x27, local copies, waits for them, and re-layouts  45.6 us
    pmax x1, blocking collectives, per_device(): rows_mine = lax.pmax(local_rows_max, 'tensor')  26.4 us
    reduce_max x1, other arithmetic, per_device(): jnp.max(first_abs, axis=1)  15.6 us
    dot_general x1, matrix products, per_device(): jnp.einsum('sc,sh->ch', block, attended, preferred_element_type=jnp.float32)  14.5 us
    dot_general x1, matrix products, per_device(): jnp.dot(block, lax.all_gather(weight_half, 'dp', axis=0, tiled=True), pre...  12.1 us
  transfers between devices with their start and end apart: 3, of which 3 were waited for; matrix products, arithmetic and copies ran while one was open for 7% of the time, Pallas kernels for 0%

commit v1 on v0

--- a/solution.py
+++ b/solution.py
@@ -14,6 +14,22 @@
 code_eps = 1e-06
 correct_first = 1.0 - 0.9**10
 correct_second = 1.0 - 0.95**10
+
+
+def supply_all_the_pieces_all(w_in):
+    amount_of = lax.axis_size("tensor")
+    rows = []
+    for dev in tuple(range(1, amount_of)):
+        rows.append((dev - 1, dev))
+    z1 = rows + [(amount_of - 1, 0)]
+    lower = w_in
+    row_list = [lower]
+    for _ in tuple(range(amount_of - 1)):
+        lower = lax.ppermute(lower, "tensor", z1)
+        row_list += [lower]
+    val2 = jnp.concatenate([*reversed(row_list)], axis=1)
+    t_next = lax.axis_index("tensor")
+    return jnp.roll(val2, (t_next + 1) * lower.shape[1], axis=1)
 
 
 def attend(queries, key_sel, value_sel, heads_dev):
@@ -75,7 +91,7 @@
     tensor_index = lax.axis_index("tensor")
     kv_start = tensor_index * heads_dev // (H // KVH) * HD
     weight_half = weight.astype(jnp.bfloat16)
-    full_grad = lax.all_gather(grad_out, "tensor", axis=1, tiled=True)
+    full_grad = supply_all_the_pieces_all(grad_out)
     padded = jnp.pad(full_grad, ((0, 0), (0, width_pad - full_grad.shape[1])))
     key_sel = lax.dynamic_slice_in_dim(keys, kv_start, HD, 1)
     value_sel = lax.dynamic_slice_in_dim(values, kv_start, HD, 1)

time: 512 us -> 486 us (0.949)
  local copies, waits for them, and re-layouts: 46 us -> 14.7 us
    ppermute x0 -> x7, waiting for transfers between devices: none -> 85.3 us  [supply_all_the_pieces_all(): lower = lax.ppermute(lower, 'tensor', z1)]
    all_gather x1 -> x0, waiting for transfers between devices: 58.3 us -> none  [per_device(): full_grad = lax.all_gather(grad_out, 'tensor', axis=1, tiled=True)]
    all_gather x1, waiting for transfers between devices: 158 us -> 111 us  [per_device(): lax.all_gather(weight_half, 'dp', axis=0, tiled=True)]
    unnamed x27 -> x46, local copies, waits for them, and re-layouts: 45.6 us -> 14.3 us
    reduce_scatter x1, waiting for transfers between devices: 127 us -> 152 us  [per_device(): lax.psum_scatter(jnp.einsum('sc,sh->ch', block, attended, preferred_eleme...]
    convert_element_type x1 -> x0, other arithmetic: 6.13 us -> none  [per_device(): weight_half = weight.astype(jnp.bfloat16)]
    reduce_max x1, other arithmetic: 15.6 us -> 20.8 us  [per_device(): jnp.max(first_abs, axis=1)]
  transfers between devices with their start and end apart: 3 -> 9, of which waited for: 3 -> 9; matrix products, arithmetic and copies ran while one was open for 7% -> 4% of each run, Pallas kernels for 0% -> 0%
where the time goes in v1:
time: 486 us
  waiting for transfers between devices  348 us (72%)
  matrix products  36.2 us (7%)
  other arithmetic  35.7 us (7%)
  blocking collectives  35.4 us (7%)
  local copies, waits for them, and re-layouts  14.7 us (3%)
  between operations  14.4 us (3%)
    reduce_scatter x1, waiting for transfers between devices, per_device(): lax.psum_scatter(jnp.einsum('sc,sh->ch', block, attended, preferred_eleme...  152 us
    all_gather x1, waiting for transfers between devices, per_device(): lax.all_gather(weight_half, 'dp', axis=0, tiled=True)  111 us
    ppermute x7, waiting for transfers between devices, supply_all_the_pieces_all(): lower = lax.ppermute(lower, 'tensor', z1)  85.3 us
    pmax x1, blocking collectives, per_device(): rows_mine = lax.pmax(local_rows_max, 'tensor')  26.3 us
    reduce_max x1, other arithmetic, per_device(): jnp.max(first_abs, axis=1)  20.8 us
    dot_general x1, matrix products, per_device(): jnp.einsum('sc,sh->ch', block, attended, preferred_element_type=jnp.float32)  15.3 us
    unnamed x46, local copies, waits for them, and re-layouts  14.3 us
    dot_general x1, matrix products, per_device(): jnp.dot(block, lax.all_gather(weight_half, 'dp', axis=0, tiled=True), pre...  12.2 us
  transfers between devices with their start and end apart: 9, of which 9 were waited for; matrix products, arithmetic and copies ran while one was open for 4% of the time, Pallas kernels for 0%

profile of v1, /device:TPU:0, one launch (start us, length us, event | category | flops | bytes accessed | tf_op | source)
XLA Modules:
  0.0 485.7 jit_solution(14511362511993969023)
XLA Ops:
  7.2 0.0 copy-start
  7.2 0.0 reduce-scatter.2.cloned.1.call-start
  7.2 0.5 collective-permute-start
  7.8 13.9 %collective-permute-done = bf16[384,1024]{1,0:T(8,128)(2,1)S(1)} collective-permute-done((bf16[384,1024]{1,0:T(8,128)(2,1)}, bf16[384,1024]{1,0:T(8,128)(2,1)S(1)}, u32[]{:S(2)}, u32[]{:S(2)}) %collective-permute-start) | collective-permute-done | bytes 786464 | tf_op jit(solution)/shard_map/ppermute | solution.py:28
  21.7 0.0 collective-permute-start.1
  21.7 13.2 %collective-permute-done.1 = bf16[384,1024]{1,0:T(8,128)(2,1)S(1)} collective-permute-done((bf16[384,1024]{1,0:T(8,128)(2,1)S(1)}, bf16[384,1024]{1,0:T(8,128)(2,1)S(1)}, u32[]{:S(2)}, u32[]{:S(2)}) %collective-permute-start.1) | collective-permute-done | bytes 786464 | tf_op jit(solution)/shard_map/ppermute | solution.py:28
  34.9 0.0 collective-permute-start.2
  34.9 13.2 %collective-permute-done.2 = bf16[384,1024]{1,0:T(8,128)(2,1)S(1)} collective-permute-done((bf16[384,1024]{1,0:T(8,128)(2,1)S(1)}, bf16[384,1024]{1,0:T(8,128)(2,1)S(1)}, u32[]{:S(2)}, u32[]{:S(2)}) %collective-permute-start.2) | collective-permute-done | bytes 786464 | tf_op jit(solution)/shard_map/ppermute | solution.py:28
  48.1 0.0 collective-permute-start.3
  48.1 13.2 %collective-permute-done.3 = bf16[384,1024]{1,0:T(8,128)(2,1)S(1)} collective-permute-done((bf16[384,1024]{1,0:T(8,128)(2,1)S(1)}, bf16[384,1024]{1,0:T(8,128)(2,1)S(1)}, u32[]{:S(2)}, u32[]{:S(2)}) %collective-permute-start.3) | collective-permute-done | bytes 786464 | tf_op jit(solution)/shard_map/ppermute | solution.py:28
  61.3 0.9 copy-done.2
  62.2 0.0 collective-permute-start.4
  62.2 13.3 %collective-permute-done.4 = bf16[384,1024]{1,0:T(8,128)(2,1)} collective-permute-done((bf16[384,1024]{1,0:T(8,128)(2,1)S(1)}, bf16[384,1024]{1,0:T(8,128)(2,1)}, u32[]{:S(2)}, u32[]{:S(2)}) %collective-permute-start.4) | collective-permute-done | bytes 786464 | tf_op jit(solution)/shard_map/ppermute | solution.py:28
  75.5 0.0 collective-permute-start.5
  75.6 0.0 copy-done
  75.6 1.9 fusion.27
  77.5 11.5 %collective-permute-done.5 = bf16[384,1024]{1,0:T(8,128)(2,1)} collective-permute-done((bf16[384,1024]{1,0:T(8,128)(2,1)}, bf16[384,1024]{1,0:T(8,128)(2,1)}, u32[]{:S(2)}, u32[]{:S(2)}) %collective-permute-start.5) | collective-permute-done | bytes 786464 | tf_op jit(solution)/shard_map/ppermute | solution.py:28
  89.1 0.0 collective-permute-start.6
  89.1 3.6 fusion.50
  92.6 3.1 fusion.21
  95.7 0.0 copy-start.4
  95.7 0.0 copy-start.1
  95.7 6.8 %collective-permute-done.6 = bf16[384,1024]{1,0:T(8,128)(2,1)} collective-permute-done((bf16[384,1024]{1,0:T(8,128)(2,1)}, bf16[384,1024]{1,0:T(8,128)(2,1)}, u32[]{:S(2)}, u32[]{:S(2)}) %collective-permute-start.6) | collective-permute-done | bytes 786464 | tf_op jit(solution)/shard_map/ppermute | solution.py:28
  102.6 1.2 constant_dynamic-update-slice_fusion.15
  103.8 1.2 constant_dynamic-update-slice_fusion.14
  105.0 1.2 constant_dynamic-update-slice_fusion.13
  106.1 0.0 copy-done.3
  106.2 0.1 constant_dynamic-update-slice_fusion.12
  106.2 0.1 constant_dynamic-update-slice_fusion.11
  106.3 0.1 constant_dynamic-update-slice_fusion.10
  106.3 0.1 constant_dynamic-update-slice_fusion.9
  106.4 0.0 copy-done.1
  106.4 0.1 constant_dynamic-update-slice_fusion.8
  106.5 1.2 constant_dynamic-update-slice_fusion.7
  107.7 1.2 constant_dynamic-update-slice_fusion.6
  108.9 1.2 constant_dynamic-update-slice_fusion.5
  110.0 0.1 constant_dynamic-update-slice_fusion.4
  110.1 0.1 constant_dynamic-update-slice_fusion.3
  110.2 0.1 constant_dynamic-update-slice_fusion.2
  110.2 0.1 constant_dynamic-update-slice_fusion.1
  110.3 0.1 constant_dynamic-update-slice_fusion
  110.4 0.0 copy-start.6
  110.4 4.5 copy-done.6
  114.9 15.3 %convolution_convert_fusion = bf16[8192,1024]{1,0:T(8,128)(2,1)} fusion(bf16[384,1024]{0,1:T(8,128)(2,1)S(1)} %bitcast.63, bf16[384,16384]{1,0:T(8,128)(2,1)} %copy-done.6, s32[]{:T(128)S(6)} %select_n.29), kind=kOutput, calls=%fused_computation.1 | convolution fusion | flops 6450839552 | bytes 23855108 | tf_op jit(solution)/shard_map/sc,sh->ch/dot_general | solution.py:107
  130.3 0.0 reduce-scatter.2.cloned.1.call-update
  130.3 0.2 all-gather.2.cloned.1.call-start
  130.5 152.4 %reduce-scatter.2.cloned.1.call-done = bf16[2048,1024]{1,0:T(8,128)(2,1)} async-done(((bf16[8192,1024]{1,0:T(8,128)(2,1)}), bf16[2048,1024]{1,0:T(8,128)(2,1)}) %reduce-scatter.2.cloned.1.call-update) | async-done | bytes 4194320 | tf_op jit(solution)/shard_map/reduce_scatter | solution.py:106
  282.9 0.0 copy-done.12
  282.9 20.8 %abs_reduce_fusion.3 = (f32[2048]{0:T(1024)S(1)}, f32[1024]{0:T(1024)S(1)}, f32[1024]{0:T(1024)S(1)}, f32[2048]{0:T(1024)S(1)}, f32[2048,1024]{1,0:T(8,128)}, /*index=5*/bf16[2048,1024]{1,0:T(8,128)(2,1)}) fusion(bf16[2048,1024]{1,0:T(8,128)(2,1)} %reduce-scatter.2.cloned.1.call-done, f32[1024]{0:T(1024)S(1)} %copy-done.11, f32[2048]{0:T(1024)S(1)} %copy-done.7, ...), kind=kLoop, calls=%fused_computation.12 | loop fusion | flops 60811264 | bytes 33603584 | tf_op jit(solution)/shard_map/reduce_max | solution.py:126
  303.7 0.0 all-gather.2.cloned.1.call-update
  303.8 9.1 %pmax.15 = f32[2,1024]{1,0:T(2,128)S(1)} all-reduce(f32[2,1024]{1,0:T(2,128)S(1)} %pad_maximum_fusion.1), channel_id=1, replica_groups=mesh['dp'=4,'tensor'=8] {'dp'}, use_global_device_ids=true, to_apply=%region_9.10 | all-reduce | flops 2048 | bytes 16384 | tf_op jit(solution)/shard_map/pmax | solution.py:129
  312.9 26.3 %pmax.14 = f32[2,2048]{1,0:T(2,128)S(1)} all-reduce(f32[2,2048]{1,0:T(2,128)S(1)} %pad_maximum_fusion), channel_id=1, replica_groups=mesh['dp'=4,'tensor'=8] {'tensor'}, use_global_device_ids=true, to_apply=%region_6.7 | all-reduce | flops 4096 | bytes 32768 | tf_op jit(solution)/shard_map/pmax | solution.py:128
  339.2 0.0 copy-start.13
  339.3 0.0 copy-start.14
  339.3 0.0 copy-start.9
  339.3 0.0 copy-start.10
  339.3 11.0 %divide_convert_fusion = (bf16[2048,1024]{1,0:T(8,128)(2,1)}, bf16[2048,1024]{1,0:T(8,128)(2,1)}) fusion(f32[1024]{0:T(1024)S(1)} %bitcast.71, f32[2048]{0:T(1024)S(1)} %bitcast.65, bf16[2048,1024]{1,0:T(8,128)(2,1)} %reduce-scatter.2.cloned.1.call-done, f32[1024]{0:T(1024)S(1)} %copy-done.12, f32[2048]{0:T(1024)S(1)} %copy-done.8, ...), kind=kLoop, calls=%fused_computation.6 | loop fusion | flops 46137344 | bytes 21020672 | tf_op jit(solution)/shard_map/convert_element_type | solution.py:135
  350.3 0.0 copy-done.13
  350.4 110.8 %all-gather.2.cloned.1.call-done = bf16[8192,1024]{1,0:T(8,128)(2,1)} async-done(((bf16[2048,1024]{1,0:T(8,128)(2,1)}), bf16[8192,1024]{1,0:T(8,128)(2,1)}) %all-gather.2.cloned.1.call-update) | async-done | bytes 16777232 | tf_op jit(solution)/shard_map/all_gather | solution.py:102
  461.2 12.2 %fusion.24 = bf16[384,1024]{1,0:T(8,128)(2,1)S(1)} fusion(bf16[8192,1024]{1,0:T(8,128)(2,1)} %all-gather.2.cloned.1.call-done, bf16[384,16384]{1,0:T(8,128)(2,1)} %copy-done.6, s32[]{:T(128)S(6)} %select_n.29), kind=kOutput, calls=%fused_computation.34 | convolution fusion | flops 6442844160 | bytes 23855108 | tf_op jit(solution)/shard_map/dot_general | solution.py:100
  473.4 0.4 copy.30
  473.8 0.2 multiply_reduce_fusion
  474.0 3.6 multiply_convert_fusion
  477.7 1.2 copy.25
  (20 shorter events, 0.1 us)
Async XLA Ops:
  7.2 68.4 %copy-start = (bf16[384,1024]{1,0:T(8,128)(2,1)S(1)}, bf16[384,1024]{1,0:T(8,128)(2,1)}, u32[]{:S(2)}) copy-start(bf16[384,1024]{1,0:T(8,128)(2,1)} %param.12) | copy-start | bytes 2359300
  7.2 275.7 %reduce-scatter.2.cloned.1.call-start = ((), (), s32[]{:S(2)}) async-start(), calls=%async_computation.2 | async-start | bytes 20971520 | tf_op jit(solution)/shard_map/reduce_scatter | solution.py:106
  7.2 14.5 %collective-permute-start = (bf16[384,1024]{1,0:T(8,128)(2,1)}, bf16[384,1024]{1,0:T(8,128)(2,1)S(1)}, u32[]{:S(2)}, u32[]{:S(2)}) collective-permute-start(bf16[384,1024]{1,0:T(8,128)(2,1)} %param.14), channel_id=1, source_target_pairs={{0,1},{1,2},{2,3},{3,4},{4,5},{5,6},{6,7},{7,0},{8,9},{9,10},{10,1... | collective-permute-start | bytes 2359304 | tf_op jit(solution)/shard_map/ppermute | solution.py:28
  21.7 13.2 %collective-permute-start.1 = (bf16[384,1024]{1,0:T(8,128)(2,1)S(1)}, bf16[384,1024]{1,0:T(8,128)(2,1)S(1)}, u32[]{:S(2)}, u32[]{:S(2)}) collective-permute-start(bf16[384,1024]{1,0:T(8,128)(2,1)S(1)} %collective-permute-done), channel_id=1, source_target_pairs={{0,1},{1,2},{2,3},{3,4},{4,5},{5,6},{6,7},{7,0},{8,9},{9,10},{10,1... | collective-permute-start | bytes 2359304 | tf_op jit(solution)/shard_map/ppermute | solution.py:28
  34.9 13.2 %collective-permute-start.2 = (bf16[384,1024]{1,0:T(8,128)(2,1)S(1)}, bf16[384,1024]{1,0:T(8,128)(2,1)S(1)}, u32[]{:S(2)}, u32[]{:S(2)}) collective-permute-start(bf16[384,1024]{1,0:T(8,128)(2,1)S(1)} %collective-permute-done.1), channel_id=1, source_target_pairs={{0,1},{1,2},{2,3},{3,4},{4,5},{5,6},{6,7},{7,0},{8,9},{9,10},{10,1... | collective-permute-start | bytes 2359304 | tf_op jit(solution)/shard_map/ppermute | solution.py:28
  48.1 13.2 %collective-permute-start.3 = (bf16[384,1024]{1,0:T(8,128)(2,1)S(1)}, bf16[384,1024]{1,0:T(8,128)(2,1)S(1)}, u32[]{:S(2)}, u32[]{:S(2)}) collective-permute-start(bf16[384,1024]{1,0:T(8,128)(2,1)S(1)} %collective-permute-done.2), channel_id=1, source_target_pairs={{0,1},{1,2},{2,3},{3,4},{4,5},{5,6},{6,7},{7,0},{8,9},{9,10},{10,1... | collective-permute-start | bytes 2359304 | tf_op jit(solution)/shard_map/ppermute | solution.py:28
  61.3 0.9 copy-start.2
  62.2 13.3 %collective-permute-start.4 = (bf16[384,1024]{1,0:T(8,128)(2,1)S(1)}, bf16[384,1024]{1,0:T(8,128)(2,1)}, u32[]{:S(2)}, u32[]{:S(2)}) collective-permute-start(bf16[384,1024]{1,0:T(8,128)(2,1)S(1)} %collective-permute-done.3), channel_id=1, source_target_pairs={{0,1},{1,2},{2,3},{3,4},{4,5},{5,6},{6,7},{7,0},{8,9},{9,10},{10,1... | collective-permute-start | bytes 2359304 | tf_op jit(solution)/shard_map/ppermute | solution.py:28
  75.5 13.5 %collective-permute-start.5 = (bf16[384,1024]{1,0:T(8,128)(2,1)}, bf16[384,1024]{1,0:T(8,128)(2,1)}, u32[]{:S(2)}, u32[]{:S(2)}) collective-permute-start(bf16[384,1024]{1,0:T(8,128)(2,1)} %collective-permute-done.4), channel_id=1, source_target_pairs={{0,1},{1,2},{2,3},{3,4},{4,5},{5,6},{6,7},{7,0},{8,9},{9,10},{10,1... | collective-permute-start | bytes 2359304 | tf_op jit(solution)/shard_map/ppermute | solution.py:28
  89.1 13.5 %collective-permute-start.6 = (bf16[384,1024]{1,0:T(8,128)(2,1)}, bf16[384,1024]{1,0:T(8,128)(2,1)}, u32[]{:S(2)}, u32[]{:S(2)}) collective-permute-start(bf16[384,1024]{1,0:T(8,128)(2,1)} %collective-permute-done.5), channel_id=1, source_target_pairs={{0,1},{1,2},{2,3},{3,4},{4,5},{5,6},{6,7},{7,0},{8,9},{9,10},{10,1... | collective-permute-start | bytes 2359304 | tf_op jit(solution)/shard_map/ppermute | solution.py:28
  92.6 13.5 %copy-start.3 = (bf16[384,1024]{1,0:T(8,128)(2,1)S(1)}, bf16[384,1024]{1,0:T(8,128)(2,1)}, u32[]{:S(2)}) copy-start(bf16[384,1024]{1,0:T(8,128)(2,1)} %copy-done.2) | copy-start | bytes 2359300
  95.7 19.2 %copy-start.4 = (bf16[128,8,384]{2,0,1:T(8,128)(2,1)}, bf16[128,8,384]{2,0,1:T(8,128)(2,1)S(1)}, u32[]{:S(2)}) copy-start(bf16[128,8,384]{2,0,1:T(8,128)(2,1)S(1)} %fusion.21) | copy-start | bytes 2359300
  95.7 10.7 %copy-start.1 = (bf16[384,1024]{1,0:T(8,128)(2,1)S(1)}, bf16[384,1024]{1,0:T(8,128)(2,1)}, u32[]{:S(2)}) copy-start(bf16[384,1024]{1,0:T(8,128)(2,1)} %param.14) | copy-start | bytes 2359300
  110.4 4.5 copy-start.6
  130.2 152.6 %copy-start.7 = (f32[2048]{0:T(1024)S(1)}, f32[2048]{0:T(1024)}, u32[]{:S(2)}) copy-start(f32[2048]{0:T(1024)} %param.17) | copy-start | bytes 24580
  130.3 152.6 %copy-start.8 = (f32[2048]{0:T(1024)S(1)}, f32[2048]{0:T(1024)}, u32[]{:S(2)}) copy-start(f32[2048]{0:T(1024)} %param.20) | copy-start | bytes 24580
  130.3 152.6 %copy-start.11 = (f32[1024]{0:T(1024)S(1)}, f32[1024]{0:T(1024)}, u32[]{:S(2)}) copy-start(f32[1024]{0:T(1024)} %param.18) | copy-start | bytes 12292
  130.3 152.6 %copy-start.12 = (f32[1024]{0:T(1024)S(1)}, f32[1024]{0:T(1024)}, u32[]{:S(2)}) copy-start(f32[1024]{0:T(1024)} %param.21) | copy-start | bytes 12292
  130.3 330.9 %all-gather.2.cloned.1.call-start = ((), (), s32[]{:S(2)}) async-start(), calls=%async_computation.1 | async-start | bytes 20971520 | tf_op jit(solution)/shard_map/all_gather | solution.py:102
  339.2 11.1 %copy-start.13 = (f32[1,1024]{1,0:T(1,128)}, f32[1,1024]{1,0:T(1,128)S(1)}, u32[]{:S(2)}) copy-start(f32[1,1024]{1,0:T(1,128)S(1)} %get-tuple-element.28) | copy-start | bytes 12292
  339.3 11.1 %copy-start.14 = (f32[1,1024]{1,0:T(1,128)}, f32[1,1024]{1,0:T(1,128)S(1)}, u32[]{:S(2)}) copy-start(f32[1,1024]{1,0:T(1,128)S(1)} %get-tuple-element.29) | copy-start | bytes 12292
  339.3 11.0 %copy-start.9 = (f32[1,2048]{1,0:T(1,128)}, f32[1,2048]{1,0:T(1,128)S(1)}, u32[]{:S(2)}) copy-start(f32[1,2048]{1,0:T(1,128)S(1)} %get-tuple-element.26) | copy-start | bytes 24580
  339.3 11.0 %copy-start.10 = (f32[1,2048]{1,0:T(1,128)}, f32[1,2048]{1,0:T(1,128)S(1)}, u32[]{:S(2)}) copy-start(f32[1,2048]{1,0:T(1,128)S(1)} %get-tuple-element.27) | copy-start | bytes 24580
  350.3 123.4 %copy-start.5 = (bf16[128,8,384]{2,0,1:T(8,128)(2,1)S(1)}, bf16[128,8,384]{2,0,1:T(8,128)(2,1)}, u32[]{:S(2)}) copy-start(bf16[128,8,384]{2,0,1:T(8,128)(2,1)} %copy-done.4) | copy-start | bytes 2359300
Sparse Core Ops, SparseCore 0:
  130.4 152.4 reduce-scatter.1
  303.9 157.2 all-gather.1
